TPU v7x, 32 devices: a whole 2x2x4 slice. The times are simulated.
32 devices in a mesh: vid: 4 (over z), th: 4 (over x, core), tw: 2 (over y).
Axes of the slice: x: 2, y: 2, z: 4, core: 2. Of those that a mesh axis runs over, the one named last changes fastest.
Arguments:
- queries: bfloat16 [16, 32, 6, 3072], P('vid', 'th', 'tw'), parts along dimension 0, may hold values from -70 to 70
- video_kv: bfloat16 [2, 16, 32, 6, 3072], P(None, 'vid', 'th', 'tw'), parts along dimension 1, may hold values from -6 to 6
- text_kv: bfloat16 [2, 904, 3072], P(None, 'vid', 'tw'), parts along dimension 1, may hold values from -6 to 6
- time_embed: bfloat16 [2048], P('vid'), parts along dimension 0, may hold values from -6 to 6
- gate_weight: bfloat16 [512, 3072], P(None, 'tw'), may hold values from -0.25 to 0.25
- window_extent: int32 [48, 2], replicated, may hold values from 1 to 3
- tile_valid: int32 [16, 2, 2], P('vid'), parts along dimension 0, may hold values from 2 to 8, as said below
Outputs:
- gated: bfloat16 [16, 32, 6, 3072], P('vid', 'th', 'tw'), parts along dimension 0
There are 4 independent parts, one for each index of `vid`. A program takes and returns all parts, laid end to end along the dimension named above; an argument that names none is the same for every part. Nothing has to cross between parts.
Inputs may be any that keep to these rules, and one draw needn't show every extreme that they name: Tile (i, j) holds tokens in its leading tile_valid[i, j, 0] of 8 rows and leading tile_valid[i, j, 1] of 3 columns; its other slots are padding. Some tile is full in every draw.
All inputs are finite; a program needn't handle non-finite values.
Results may differ from a plain program's by a relative error of at most 0.0063.
Values may be sent and summed in bfloat16 or wider, within the bound.
A program may use at most 128 MiB of HBM per device.

v0:
```python
import functools

import jax
import jax.numpy as jnp
import numpy as np
from jax import lax
from jax.experimental import pallas as pl
from jax.experimental.pallas import tpu as pltpu
from jax.sharding import PartitionSpec as P

HEAD_DIM = 64
HALO = 3
NEG = -1e30
FAR = 1 << 20
GROUP = 128
MESH = pl.DeviceIdType.MESH


def halo_rows(tile_rows, per_row):
    for rows in range(HALO, tile_rows + 1):
        if rows * per_row % 16 == 0:
            return rows
    return tile_rows


def dot_nt(a, b):
    return lax.dot_general(a, b, (((1,), (1,)), ((), ())), preferred_element_type=jnp.float32)


def kernel(
    dims,
    ext_in,
    valid_in,
    q_in,
    kv_in,
    text_in,
    time_in,
    gw_in,
    qmeta_in,
    kmeta_in,
    perm_in,
    out_ref,
    ext_ref,
    valid_ref,
    time_ref,
    qmeta,
    kmeta,
    perm,
    qbuf,
    kvbuf,
    packed,
    obuf,
    text_raw,
    text_ref,
    gw_ref,
    gate,
    row_gap,
    col_gap,
    pre_sem,
    loc_sem,
    send_sem,
    recv_sem,
    halo_send,
    halo_recv,
    out_send,
    out_recv,
):
    n_th, n_tw, chunks, lanes, tokens, halo, tile_cols, wide, flat = dims
    span = tokens + 2 * halo
    th = lax.axis_index("th")
    tw = lax.axis_index("tw")
    own = pl.ds(halo, tokens)
    heads_per_chunk = lanes // HEAD_DIM

    def peer(i):
        return lax.rem(tw + i, n_tw)

    def source(i):
        return lax.rem(tw + n_tw - i, n_tw)

    def piece(ref, j, c):
        if flat:
            return ref.at[..., pl.ds(pl.multiple_of((j * chunks + c) * lanes, lanes), lanes)]
        return ref.at[j, c]

    def remote(src, dst, ssem, rsem, where):
        return pltpu.make_async_remote_copy(
            src_ref=src, dst_ref=dst, send_sem=ssem, recv_sem=rsem, device_id=where, device_id_type=MESH
        )

    def kv_copy(c, i, slot):
        return remote(
            piece(kv_in, peer(i), c), kvbuf.at[c, slot, :, own, :], send_sem.at[c, i - 1, 0], recv_sem.at[c, i - 1, 0], {"tw": peer(i)}
        )

    def q_copy(c, i, slot):
        return remote(
            piece(q_in, peer(i), c), qbuf.at[c, slot], send_sem.at[c, i - 1, 1], recv_sem.at[c, i - 1, 1], {"tw": peer(i)}
        )

    def kv_local(c):
        return pltpu.make_async_copy(piece(kv_in, tw, c), kvbuf.at[c, tw, :, own, :], loc_sem.at[c, 0])

    def q_local(c):
        return pltpu.make_async_copy(piece(q_in, tw, c), qbuf.at[c, tw], loc_sem.at[c, 1])

    def halo_up(c, landing):
        dst = pl.ds(halo + tokens, halo)
        return remote(
            packed.at[c, :, :, pl.ds(0, halo), :], kvbuf.at[c, :, :, dst, :], halo_send.at[c, 0], halo_recv.at[c, 0], {"th": th - 1 + landing}
        )

    def halo_down(c, landing):
        dst = pl.ds(0, halo)
        return remote(
            packed.at[c, :, :, pl.ds(halo, halo), :], kvbuf.at[c, :, :, dst, :], halo_send.at[c, 1], halo_recv.at[c, 1], {"th": th + 1 - landing}
        )

    def out_copy(c, i, slot):
        return remote(obuf.at[c, peer(i)], piece(out_ref, slot, c), out_send.at[c, i - 1], out_recv.at[c, i - 1], {"tw": peer(i)})

    def out_local(c):
        return pltpu.make_async_copy(obuf.at[c, tw], piece(out_ref, tw, c), loc_sem.at[c, 2])

    has_up = th > 0
    has_down = th < n_th - 1

    barrier = pltpu.get_barrier_semaphore()
    for i in range(1, n_tw):
        pl.semaphore_signal(barrier, inc=1, device_id={"tw": peer(i)}, device_id_type=MESH)

    @pl.when(has_up)
    def _():
        pl.semaphore_signal(barrier, inc=1, device_id={"th": th - 1}, device_id_type=MESH)

    @pl.when(has_down)
    def _():
        pl.semaphore_signal(barrier, inc=1, device_id={"th": th + 1}, device_id_type=MESH)

    pl.semaphore_wait(barrier, n_tw - 1 + has_up.astype(jnp.int32) + has_down.astype(jnp.int32))

    for c in range(chunks):
        for i in range(1, n_tw):
            kv_copy(c, i, tw).start()
            q_copy(c, i, tw).start()

    gw_load = pltpu.make_async_copy(gw_in, gw_ref, pre_sem.at[0])
    text_load = pltpu.make_async_copy(text_in, text_raw, pre_sem.at[1])
    for c in range(chunks):
        kv_local(c).start()
        q_local(c).start()
    small = [
        pltpu.make_async_copy(src, dst, pre_sem.at[2 + k])
        for k, (src, dst) in enumerate(
            [
                (ext_in, ext_ref),
                (valid_in, valid_ref),
                (time_in, time_ref),
                (qmeta_in, qmeta),
                (kmeta_in, kmeta),
                (perm_in, perm),
            ]
        )
    ]
    for load in small:
        load.start()
    gw_load.start()
    text_load.start()

    @pl.when(jnp.logical_not(has_up))
    def _():
        kvbuf[:, :, :, pl.ds(0, halo), :] = jnp.zeros((chunks, n_tw, 2, halo, lanes), kvbuf.dtype)

    @pl.when(jnp.logical_not(has_down))
    def _():
        kvbuf[:, :, :, pl.ds(halo + tokens, halo), :] = jnp.zeros((chunks, n_tw, 2, halo, lanes), kvbuf.dtype)

    def find_gate():
        time = time_ref[...].astype(jnp.float32)
        mod_in = (time / (1.0 + jnp.exp(-time))).astype(jnp.bfloat16)
        gw_load.wait()
        depth = mod_in.shape[1]
        gate_vec = jnp.zeros((1, chunks * lanes), jnp.float32)
        for k in range(mod_in.shape[0]):
            gate_vec = gate_vec + jnp.dot(
                mod_in[k : k + 1], gw_ref[k * depth : (k + 1) * depth], preferred_element_type=jnp.float32
            )
        gate_vec = gate_vec.astype(jnp.bfloat16).astype(jnp.float32)
        for c in range(chunks):
            gate[c] = gate_vec[:, c * lanes : (c + 1) * lanes]

    for load in small:
        load.wait()

    reach = -(-HALO // tile_cols)

    def first_tile(t):
        return jnp.clip(t - reach, 0, n_tw - wide)

    q_row = qmeta[:, 0:1]
    q_col = qmeta[:, 1:2]
    k_row = kmeta[0:1, :]
    k_band = kmeta[1:2, :]
    k_local = kmeta[2:3, :]
    k_col = kmeta[3:4, :]
    above = jnp.maximum(th - 1, 0)
    below = jnp.minimum(th + 1, n_th - 1)

    def distances(t, carry):
        start = first_tile(t)
        for j in range(wide):
            tc = start + j
            limits = []
            for what in range(2):
                up = jnp.where(has_up, valid_ref[tc, what, above], 0)
                mid = valid_ref[tc, what, th]
                down = jnp.where(has_down, valid_ref[tc, what, below], 0)
                limits.append(jnp.where(k_band == 0, up, jnp.where(k_band == 1, mid, down)))
            bad = jnp.where((k_local < limits[0]) & (k_col < limits[1]), 0, FAR)
            row_gap[t, :, pl.ds(j * span, span)] = jnp.abs(k_row - q_row) + bad
            col_gap[t, :, pl.ds(j * span, span)] = jnp.abs(k_col + (tc - t) * tile_cols - q_col)
        return carry

    lax.fori_loop(0, n_tw, distances, 0)
    find_gate()
    text_load.wait()
    for s in range(2):
        text_ref[s] = text_raw[:, s, :]

    def attend(c, t):
        start = first_tile(t)
        q_ok = (q_row < valid_ref[t, 0, th]) & (q_col < valid_ref[t, 1, th])
        rows_apart = row_gap[t]
        cols_apart = col_gap[t]
        for low in range(0, lanes, GROUP):
            width = min(GROUP, lanes - low)
            count = width // HEAD_DIM
            part = pl.ds(low, width)
            q = qbuf[c, t, :, part]
            keys = kvbuf[c, pl.ds(start, wide), 0, :, part].reshape(wide * span, width)
            values = kvbuf[c, pl.ds(start, wide), 1, :, part].reshape(wide * span, width)
            if chunks == 1:
                at = part
            else:
                at = pl.ds(pl.multiple_of(c * lanes + low, GROUP), width)
            t_keys = text_ref[0, :, at]
            t_values = text_ref[1, :, at]
            lane = lax.broadcasted_iota(jnp.int32, (1, width), 1)
            stacked = []
            for s in range(count):
                mine = (lane >= s * HEAD_DIM) & (lane < (s + 1) * HEAD_DIM)
                stacked.append(q * jnp.where(mine, HEAD_DIM ** -0.5, 0.0).astype(jnp.bfloat16))
            q_all = jnp.concatenate(stacked, axis=0) if count > 1 else stacked[0]
            scores = dot_nt(q_all, keys)
            t_scores = dot_nt(q_all, t_keys)
            weights, t_weights, inverse = [], [], []
            for s in range(count):
                head = tw * (chunks * heads_per_chunk) + c * heads_per_chunk + low // HEAD_DIM + s
                allowed = (rows_apart <= ext_ref[0, head]) & (cols_apart <= ext_ref[1, head])
                sv = jnp.where(allowed, scores[s * tokens : (s + 1) * tokens], NEG)
                st = t_scores[s * tokens : (s + 1) * tokens]
                top = jnp.maximum(jnp.max(sv, axis=-1, keepdims=True), jnp.max(st, axis=-1, keepdims=True))
                ev = jnp.exp(sv - top)
                et = jnp.exp(st - top)
                inverse.append(1.0 / (jnp.sum(ev, axis=-1, keepdims=True) + jnp.sum(et, axis=-1, keepdims=True)))
                weights.append(ev.astype(jnp.bfloat16))
                t_weights.append(et.astype(jnp.bfloat16))
            w_all = jnp.concatenate(weights, axis=0) if count > 1 else weights[0]
            tw_all = jnp.concatenate(t_weights, axis=0) if count > 1 else t_weights[0]
            mixed = jnp.dot(w_all, values, preferred_element_type=jnp.float32) + jnp.dot(
                tw_all, t_values, preferred_element_type=jnp.float32
            )
            result = mixed[0:tokens] * inverse[0]
            for s in range(1, count):
                result = jnp.where(lane >= s * HEAD_DIM, mixed[s * tokens : (s + 1) * tokens] * inverse[s], result)
            result = result * gate[c, :, part]
            obuf[c, t, :, part] = jnp.where(q_ok, result, 0.0).astype(jnp.bfloat16)

    def step(at, carry):
        @pl.when(at < chunks)
        def _():
            kv_local(at).wait()
            for i in range(1, n_tw):
                kv_copy(at, i, source(i)).wait_recv()

            def pack(j, inner):
                for s in range(2):
                    rows = jnp.dot(perm[...], kvbuf[at, j, s, own, :], preferred_element_type=jnp.float32)
                    packed[at, j, s] = rows.astype(jnp.bfloat16)
                return inner

            lax.fori_loop(0, n_tw, pack, 0)

            @pl.when(has_up)
            def _():
                halo_up(at, 0).start()

            @pl.when(has_down)
            def _():
                halo_down(at, 0).start()

        @pl.when(at > 0)
        def _():
            c = at - 1
            q_local(c).wait()
            for i in range(1, n_tw):
                q_copy(c, i, source(i)).wait_recv()

            @pl.when(has_down)
            def _():
                halo_up(c, 2).wait_recv()

            @pl.when(has_up)
            def _():
                halo_down(c, 2).wait_recv()

            def one(i, inner):
                attend(c, peer(i))
                return inner

            lax.fori_loop(1, n_tw + 1, one, 0)
            for i in range(1, n_tw):
                out_copy(c, i, tw).start()
            out_local(c).start()

        return carry

    lax.fori_loop(0, chunks + 1, step, 0)

    for c in range(chunks):
        for i in range(1, n_tw):
            kv_copy(c, i, tw).wait_send()
            q_copy(c, i, tw).wait_send()
            out_copy(c, i, tw).wait_send()
            out_copy(c, i, source(i)).wait_recv()
        out_local(c).wait()

        @pl.when(has_up)
        def _():
            halo_up(c, 0).wait_send()

        @pl.when(has_down)
        def _():
            halo_down(c, 0).wait_send()


def body(sizes, queries, video_kv, text_kv, time_embed, gate_weight, window_extent, tile_valid):
    n_th, n_tw = sizes
    frames, tile_rows, tile_cols, model_width = queries.shape
    per_row = frames * tile_cols
    tokens = tile_rows * per_row
    rows = halo_rows(tile_rows, per_row)
    halo = rows * per_row
    span = tokens + 2 * halo
    own_width = model_width // n_tw
    lanes = 2 * GROUP if own_width % (2 * GROUP) == 0 else own_width
    chunks = own_width // lanes
    wide = min(n_tw, 2 * -(-HALO // tile_cols) + 1)

    flat = lanes % GROUP == 0

    q = queries.transpose(0, 2, 1, 3).reshape(tokens, model_width)
    kv = video_kv.transpose(0, 1, 3, 2, 4).reshape(2, tokens, model_width)
    out_form = (tokens, model_width)
    if not flat:
        q = q.reshape(tokens, n_tw, chunks, lanes).transpose(1, 2, 0, 3)
        kv = kv.reshape(2, tokens, n_tw, chunks, lanes).transpose(2, 3, 0, 1, 4)
        out_form = (n_tw, chunks, tokens, lanes)

    ids = np.arange(tokens)
    q_col, q_row = ids // tile_rows % tile_cols, ids % tile_rows
    q_meta = np.stack([q_row, q_col], axis=1).astype(np.int32)
    h_ids = np.arange(halo)
    h_block, h_row = h_ids // rows, h_ids % rows
    k_row = np.concatenate([h_row - rows, q_row, h_row + tile_rows])
    k_col = np.concatenate([h_block % tile_cols, q_col, h_block % tile_cols])
    band = np.floor_divide(k_row, tile_rows) + 1
    k_meta = np.zeros((8, span), np.int32)
    k_meta[0], k_meta[1] = k_row, band
    k_meta[2], k_meta[3] = k_row - (band - 1) * tile_rows, k_col
    picks = np.concatenate([h_block * tile_rows + h_row, h_block * tile_rows + h_row + tile_rows - rows])
    perm = (picks[:, None] == ids[None, :]).astype(np.float32)
    depth = GROUP if time_embed.shape[0] % GROUP == 0 else time_embed.shape[0]

    hbm = pl.BlockSpec(memory_space=pltpu.HBM)
    others = max(n_tw - 1, 1)
    dma = pltpu.SemaphoreType.DMA
    out = pl.pallas_call(
        functools.partial(kernel, (n_th, n_tw, chunks, lanes, tokens, halo, tile_cols, wide, flat)),
        out_shape=pltpu.VMEM(out_form, jnp.bfloat16),
        in_specs=[hbm] * 10,
        out_specs=hbm,
        scratch_shapes=[
            pltpu.SMEM((2, window_extent.shape[0]), jnp.int32),
            pltpu.SMEM((n_tw, 2, n_th), jnp.int32),
            pltpu.VMEM((time_embed.shape[0] // depth, depth), jnp.bfloat16),
            pltpu.VMEM(q_meta.shape, jnp.int32),
            pltpu.VMEM(k_meta.shape, jnp.int32),
            pltpu.VMEM(perm.shape, jnp.bfloat16),
            pltpu.VMEM((chunks, n_tw, tokens, lanes), jnp.bfloat16),
            pltpu.VMEM((chunks, n_tw, 2, span, lanes), jnp.bfloat16),
            pltpu.VMEM((chunks, n_tw, 2, 2 * halo, lanes), jnp.bfloat16),
            pltpu.VMEM((chunks, n_tw, tokens, lanes), jnp.bfloat16),
            pltpu.VMEM((text_kv.shape[1], 2, text_kv.shape[2]), jnp.bfloat16),
            pltpu.VMEM(text_kv.shape, jnp.bfloat16),
            pltpu.VMEM(gate_weight.shape, jnp.bfloat16),
            pltpu.VMEM((chunks, 1, lanes), jnp.float32),
            pltpu.VMEM((n_tw, tokens, wide * span), jnp.int32),
            pltpu.VMEM((n_tw, tokens, wide * span), jnp.int32),
            dma((8,)),
            dma((chunks, 3)),
            dma((chunks, others, 2)),
            dma((chunks, others, 2)),
            dma((chunks, 2)),
            dma((chunks, 2)),
            dma((chunks, others)),
            dma((chunks, others)),
        ],
        compiler_params=pltpu.CompilerParams(
            collective_id=0, has_side_effects=True, vmem_limit_bytes=56 * 1024 * 1024
        ),
    )(
        window_extent.T,
        tile_valid.transpose(1, 2, 0),
        q,
        kv,
        text_kv.transpose(1, 0, 2),
        time_embed.reshape(-1, depth),
        gate_weight,
        jnp.asarray(q_meta),
        jnp.asarray(k_meta),
        jnp.asarray(perm, jnp.bfloat16),
    )
    if not flat:
        out = out.transpose(2, 0, 1, 3)
    return out.reshape(frames, tile_cols, tile_rows, model_width).transpose(0, 2, 1, 3)


def solution(mesh):
    placed = (
        P("vid", "th", "tw", None),
        P(None, "vid", "th", "tw", None),
        P(None, "vid", "tw"),
        P("vid"),
        P(None, "tw"),
        P(),
        P("vid", None, None),
    )
    return jax.shard_map(
        functools.partial(body, (mesh.shape["th"], mesh.shape["tw"])),
        mesh=mesh,
        in_specs=placed,
        out_specs=P("vid", "th", "tw", None),
        check_vma=False,
    )
```

profile of v0, /device:TPU:1, one launch (start us, length us, event | category | flops | bytes accessed | tf_op | source)
XLA Modules:
  0.0 33.4 jit_solution(14656403024410681777)
XLA Ops:
  0.0 32.6 %shard_map.100 = bf16[96,3072]{1,0:T(8,128)(2,1)S(1)} custom-call(s32[2,48]{1,0:T(2,128)} %bitcast.18, s32[2,2,4]{2,1,0:T(2,128)} %bitcast.17, bf16[96,3072]{1,0:T(8,128)(2,1)} %bitcast.16, bf16[2,96,3072]{2,1,0:T(8,128)(2,1)} %bitcast.15, bf16[226,2,1536]{2,1,0:T(2,128)(2,1)} %bitcast.14, bf16[4,128]{1,0:T(4,128)(2,1)} %bitcast.19, ...), custom_call_target="tpu_custom_call" | custom-call | tf_op jit(solution)/shard_map/pallas_call | solution.py:388
  32.6 0.8 %copy.12 = bf16[4,8,3,3072]{3,1,2,0:T(8,128)(2,1)} copy(bf16[4,8,3,3072]{3,1,2,0:T(8,128)(2,1)S(1)} %bitcast.13) | data formatting | bytes 1179648
where the time goes:
time: 33.5 us; the launch traced here: 33.4 us
  Pallas kernels  32.6 us (97%)
  local copies, waits for them, and re-layouts  0.82 us (2%)
    pallas_call x1, Pallas kernels, body(): pl.pallas_call(functools.partial(kernel, (n_th, n_tw, chunks, lanes, toke...  32.6 us
    unnamed x1, local copies, waits for them, and re-layouts  0.82 us

commit v1 on v0

--- a/solution.py
+++ b/solution.py
@@ -142,6 +142,8 @@
     for c in range(chunks):
         for i in range(1, n_tw):
             kv_copy(c, i, tw).start()
+    for c in range(chunks):
+        for i in range(1, n_tw):
             q_copy(c, i, tw).start()
 
     gw_load = pltpu.make_async_copy(gw_in, gw_ref, pre_sem.at[0])
@@ -276,6 +278,8 @@
             result = result * gate[c, :, part]
             obuf[c, t, :, part] = jnp.where(q_ok, result, 0.0).astype(jnp.bfloat16)
 
+    lag = min(2, chunks)
+
     def step(at, carry):
         @pl.when(at < chunks)
         def _():
@@ -299,12 +303,10 @@
             def _():
                 halo_down(at, 0).start()
 
-        @pl.when(at > 0)
-        def _():
-            c = at - 1
+        @pl.when((at >= lag) & (at < chunks + lag))
+        def _():
+            c = at - lag
             q_local(c).wait()
-            for i in range(1, n_tw):
-                q_copy(c, i, source(i)).wait_recv()
 
             @pl.when(has_down)
             def _():
@@ -314,18 +316,28 @@
             def _():
                 halo_down(c, 2).wait_recv()
 
+        @pl.when(at >= chunks)
+        def _():
+            c = at - chunks
+            for i in range(1, n_tw):
+                q_copy(c, i, source(i)).wait_recv()
+
             def one(i, inner):
                 attend(c, peer(i))
                 return inner
 
-            lax.fori_loop(1, n_tw + 1, one, 0)
+            lax.fori_loop(1, n_tw, one, 0)
             for i in range(1, n_tw):
                 out_copy(c, i, tw).start()
-            out_local(c).start()
+
+        @pl.when((at >= lag) & (at < chunks + lag))
+        def _():
+            attend(at - lag, tw)
+            out_local(at - lag).start()
 
         return carry
 
-    lax.fori_loop(0, chunks + 1, step, 0)
+    lax.fori_loop(0, chunks + max(chunks, lag), step, 0)
 
     for c in range(chunks):
         for i in range(1, n_tw):

time: 33.5 us -> 32.8 us (0.979); the launches traced: 33.4 us -> 32.3 us
  Pallas kernels: 32.6 us -> 31.5 us
    pallas_call x1, Pallas kernels: 32.6 us -> 31.5 us  [body(): pl.pallas_call(functools.partial(kernel, (n_th, n_tw, chunks, lanes, toke...]
where the time goes in v1:
time: 32.8 us; the launch traced here: 32.3 us
  Pallas kernels  31.5 us (96%)
  local copies, waits for them, and re-layouts  0.82 us (2%)
    pallas_call x1, Pallas kernels, body(): pl.pallas_call(functools.partial(kernel, (n_th, n_tw, chunks, lanes, toke...  31.5 us
    unnamed x1, local copies, waits for them, and re-layouts  0.82 us

profile of v1, /device:TPU:1, one launch (start us, length us, event | category | flops | bytes accessed | tf_op | source)
XLA Modules:
  0.0 32.3 jit_solution(18412821313502161046)
XLA Ops:
  0.0 31.5 %shard_map.100 = bf16[96,3072]{1,0:T(8,128)(2,1)S(1)} custom-call(s32[2,48]{1,0:T(2,128)} %bitcast.18, s32[2,2,4]{2,1,0:T(2,128)} %bitcast.17, bf16[96,3072]{1,0:T(8,128)(2,1)} %bitcast.16, bf16[2,96,3072]{2,1,0:T(8,128)(2,1)} %bitcast.15, bf16[226,2,1536]{2,1,0:T(2,128)(2,1)} %bitcast.14, bf16[4,128]{1,0:T(4,128)(2,1)} %bitcast.19, ...), custom_call_target="tpu_custom_call" | custom-call | tf_op jit(solution)/shard_map/pallas_call | solution.py:400
  31.5 0.8 %copy.12 = bf16[4,8,3,3072]{3,1,2,0:T(8,128)(2,1)} copy(bf16[4,8,3,3072]{3,1,2,0:T(8,128)(2,1)S(1)} %bitcast.13) | data formatting | bytes 1179648

commit v2 on v1

--- a/solution.py
+++ b/solution.py
@@ -226,8 +226,6 @@
     lax.fori_loop(0, n_tw, distances, 0)
     find_gate()
     text_load.wait()
-    for s in range(2):
-        text_ref[s] = text_raw[:, s, :]
 
     def attend(c, t):
         start = first_tile(t)
@@ -241,12 +239,8 @@
             q = qbuf[c, t, :, part]
             keys = kvbuf[c, pl.ds(start, wide), 0, :, part].reshape(wide * span, width)
             values = kvbuf[c, pl.ds(start, wide), 1, :, part].reshape(wide * span, width)
-            if chunks == 1:
-                at = part
-            else:
-                at = pl.ds(pl.multiple_of(c * lanes + low, GROUP), width)
-            t_keys = text_ref[0, :, at]
-            t_values = text_ref[1, :, at]
+            t_keys = text_ref[c, 0, :, part]
+            t_values = text_ref[c, 1, :, part]
             lane = lax.broadcasted_iota(jnp.int32, (1, width), 1)
             stacked = []
             for s in range(count):
@@ -280,6 +274,15 @@
 
     lag = min(2, chunks)
 
+    def halos_here(c):
+        @pl.when(has_down)
+        def _():
+            halo_up(c, 2).wait_recv()
+
+        @pl.when(has_up)
+        def _():
+            halo_down(c, 2).wait_recv()
+
     def step(at, carry):
         @pl.when(at < chunks)
         def _():
@@ -303,22 +306,18 @@
             def _():
                 halo_down(at, 0).start()
 
-        @pl.when((at >= lag) & (at < chunks + lag))
-        def _():
-            c = at - lag
-            q_local(c).wait()
-
-            @pl.when(has_down)
+            mine = slice(None) if chunks == 1 else pl.ds(pl.multiple_of(at * lanes, lanes), lanes)
+            for s in range(2):
+                text_ref[at, s] = text_raw[:, s, mine]
+
+        @pl.when((at >= chunks) & (at < 2 * chunks))
+        def _():
+            c = at - chunks
+
+            @pl.when(c >= chunks - lag)
             def _():
-                halo_up(c, 2).wait_recv()
-
-            @pl.when(has_up)
-            def _():
-                halo_down(c, 2).wait_recv()
-
-        @pl.when(at >= chunks)
-        def _():
-            c = at - chunks
+                halos_here(c)
+
             for i in range(1, n_tw):
                 q_copy(c, i, source(i)).wait_recv()
 
@@ -330,14 +329,21 @@
             for i in range(1, n_tw):
                 out_copy(c, i, tw).start()
 
-        @pl.when((at >= lag) & (at < chunks + lag))
-        def _():
-            attend(at - lag, tw)
-            out_local(at - lag).start()
+        @pl.when(((at >= lag) & (at < chunks)) | (at >= 2 * chunks))
+        def _():
+            c = jnp.where(at < chunks, at - lag, at - chunks - lag)
+
+            @pl.when(at < chunks)
+            def _():
+                halos_here(c)
+
+            q_local(c).wait()
+            attend(c, tw)
+            out_local(c).start()
 
         return carry
 
-    lax.fori_loop(0, chunks + max(chunks, lag), step, 0)
+    lax.fori_loop(0, 2 * chunks + lag, step, 0)
 
     for c in range(chunks):
         for i in range(1, n_tw):
@@ -414,7 +420,7 @@
             pltpu.VMEM((chunks, n_tw, 2, 2 * halo, lanes), jnp.bfloat16),
             pltpu.VMEM((chunks, n_tw, tokens, lanes), jnp.bfloat16),
             pltpu.VMEM((text_kv.shape[1], 2, text_kv.shape[2]), jnp.bfloat16),
-            pltpu.VMEM(text_kv.shape, jnp.bfloat16),
+            pltpu.VMEM((chunks, 2, text_kv.shape[1], lanes), jnp.bfloat16),
             pltpu.VMEM(gate_weight.shape, jnp.bfloat16),
             pltpu.VMEM((chunks, 1, lanes), jnp.float32),
             pltpu.VMEM((n_tw, tokens, wide * span), jnp.int32),

time: 32.8 us -> 31.8 us (0.970)
  Pallas kernels: 31.5 us -> 30.4 us
    pallas_call x1, Pallas kernels: 31.5 us -> 30.4 us  [body(): pl.pallas_call(functools.partial(kernel, (n_th, n_tw, chunks, lanes, toke...]
where the time goes in v2:
time: 31.8 us; the launch traced here: 31.2 us
  Pallas kernels  30.4 us (96%)
  local copies, waits for them, and re-layouts  0.82 us (3%)
    pallas_call x1, Pallas kernels, body(): pl.pallas_call(functools.partial(kernel, (n_th, n_tw, chunks, lanes, toke...  30.4 us
    unnamed x1, local copies, waits for them, and re-layouts  0.82 us

profile of v2, /device:TPU:1, one launch (start us, length us, event | category | flops | bytes accessed | tf_op | source)
XLA Modules:
  0.0 31.2 jit_solution(2291075000373125571)
XLA Ops:
  0.0 30.4 %shard_map.100 = bf16[96,3072]{1,0:T(8,128)(2,1)S(1)} custom-call(s32[2,48]{1,0:T(2,128)} %bitcast.18, s32[2,2,4]{2,1,0:T(2,128)} %bitcast.17, bf16[96,3072]{1,0:T(8,128)(2,1)} %bitcast.16, bf16[2,96,3072]{2,1,0:T(8,128)(2,1)} %bitcast.15, bf16[226,2,1536]{2,1,0:T(2,128)(2,1)} %bitcast.14, bf16[4,128]{1,0:T(4,128)(2,1)} %bitcast.19, ...), custom_call_target="tpu_custom_call" | custom-call | tf_op jit(solution)/shard_map/pallas_call | solution.py:406
  30.4 0.8 %copy.12 = bf16[4,8,3,3072]{3,1,2,0:T(8,128)(2,1)} copy(bf16[4,8,3,3072]{3,1,2,0:T(8,128)(2,1)S(1)} %bitcast.13) | data formatting | bytes 1179648

commit v3 on v2

--- a/solution.py
+++ b/solution.py
@@ -58,8 +58,10 @@
     col_gap,
     pre_sem,
     loc_sem,
-    send_sem,
-    recv_sem,
+    kv_send,
+    q_send,
+    kv_recv,
+    q_recv,
     halo_send,
     halo_recv,
     out_send,
@@ -90,37 +92,37 @@
 
     def kv_copy(c, i, slot):
         return remote(
-            piece(kv_in, peer(i), c), kvbuf.at[c, slot, :, own, :], send_sem.at[c, i - 1, 0], recv_sem.at[c, i - 1, 0], {"tw": peer(i)}
+            piece(kv_in, peer(i), c), kvbuf.at[c, slot, :, own, :], kv_send.at[i - 1], kv_recv.at[c, i - 1], {"tw": peer(i)}
         )
 
     def q_copy(c, i, slot):
         return remote(
-            piece(q_in, peer(i), c), qbuf.at[c, slot], send_sem.at[c, i - 1, 1], recv_sem.at[c, i - 1, 1], {"tw": peer(i)}
+            piece(q_in, peer(i), c), qbuf.at[c, slot], q_send.at[i - 1], q_recv.at[c, i - 1], {"tw": peer(i)}
         )
 
     def kv_local(c):
-        return pltpu.make_async_copy(piece(kv_in, tw, c), kvbuf.at[c, tw, :, own, :], loc_sem.at[c, 0])
+        return pltpu.make_async_copy(piece(kv_in, tw, c), kvbuf.at[c, tw, :, own, :], loc_sem.at[0])
 
     def q_local(c):
-        return pltpu.make_async_copy(piece(q_in, tw, c), qbuf.at[c, tw], loc_sem.at[c, 1])
+        return pltpu.make_async_copy(piece(q_in, tw, c), qbuf.at[c, tw], loc_sem.at[1])
 
     def halo_up(c, landing):
         dst = pl.ds(halo + tokens, halo)
         return remote(
-            packed.at[c, :, :, pl.ds(0, halo), :], kvbuf.at[c, :, :, dst, :], halo_send.at[c, 0], halo_recv.at[c, 0], {"th": th - 1 + landing}
+            packed.at[c, :, :, pl.ds(0, halo), :], kvbuf.at[c, :, :, dst, :], halo_send.at[0], halo_recv.at[c, 0], {"th": th - 1 + landing}
         )
 
     def halo_down(c, landing):
         dst = pl.ds(0, halo)
         return remote(
-            packed.at[c, :, :, pl.ds(halo, halo), :], kvbuf.at[c, :, :, dst, :], halo_send.at[c, 1], halo_recv.at[c, 1], {"th": th + 1 - landing}
+            packed.at[c, :, :, pl.ds(halo, halo), :], kvbuf.at[c, :, :, dst, :], halo_send.at[1], halo_recv.at[c, 1], {"th": th + 1 - landing}
         )
 
     def out_copy(c, i, slot):
-        return remote(obuf.at[c, peer(i)], piece(out_ref, slot, c), out_send.at[c, i - 1], out_recv.at[c, i - 1], {"tw": peer(i)})
+        return remote(obuf.at[c, peer(i)], piece(out_ref, slot, c), out_send.at[i - 1], out_recv.at[i - 1], {"tw": peer(i)})
 
     def out_local(c):
-        return pltpu.make_async_copy(obuf.at[c, tw], piece(out_ref, tw, c), loc_sem.at[c, 2])
+        return pltpu.make_async_copy(obuf.at[c, tw], piece(out_ref, tw, c), loc_sem.at[2])
 
     has_up = th > 0
     has_down = th < n_th - 1
@@ -139,12 +141,13 @@
 
     pl.semaphore_wait(barrier, n_tw - 1 + has_up.astype(jnp.int32) + has_down.astype(jnp.int32))
 
-    for c in range(chunks):
+    behind = chunks // 2
+    for c in range(chunks + behind):
         for i in range(1, n_tw):
-            kv_copy(c, i, tw).start()
-    for c in range(chunks):
-        for i in range(1, n_tw):
-            q_copy(c, i, tw).start()
+            if c < chunks:
+                kv_copy(c, i, tw).start()
+            if c >= behind:
+                q_copy(c - behind, i, tw).start()
 
     gw_load = pltpu.make_async_copy(gw_in, gw_ref, pre_sem.at[0])
     text_load = pltpu.make_async_copy(text_in, text_raw, pre_sem.at[1])
@@ -152,8 +155,8 @@
         kv_local(c).start()
         q_local(c).start()
     small = [
-        pltpu.make_async_copy(src, dst, pre_sem.at[2 + k])
-        for k, (src, dst) in enumerate(
+        pltpu.make_async_copy(src, dst, pre_sem.at[2])
+        for src, dst in (
             [
                 (ext_in, ext_ref),
                 (valid_in, valid_ref),
@@ -273,6 +276,10 @@
             obuf[c, t, :, part] = jnp.where(q_ok, result, 0.0).astype(jnp.bfloat16)
 
     lag = min(2, chunks)
+    early = max(0, chunks - 1 - lag)
+
+    def all_of(ref, sem):
+        pltpu.make_async_copy(ref, ref, sem).wait()
 
     def halos_here(c):
         @pl.when(has_down)
@@ -283,10 +290,12 @@
         def _():
             halo_down(c, 2).wait_recv()
 
+    all_of(kvbuf.at[:, tw, :, own, :], loc_sem.at[0])
+    all_of(qbuf.at[:, tw], loc_sem.at[1])
+
     def step(at, carry):
         @pl.when(at < chunks)
         def _():
-            kv_local(at).wait()
             for i in range(1, n_tw):
                 kv_copy(at, i, source(i)).wait_recv()
 
@@ -310,56 +319,57 @@
             for s in range(2):
                 text_ref[at, s] = text_raw[:, s, mine]
 
-        @pl.when((at >= chunks) & (at < 2 * chunks))
-        def _():
-            c = at - chunks
-
-            @pl.when(c >= chunks - lag)
+        late = at >= chunks + behind
+        own_now = ((at >= lag) & (at < lag + early)) | late
+        away_now = (at >= behind) & jnp.logical_not(late)
+        own_c = jnp.where(late, at - (chunks + behind) + early, at - lag)
+        away_c = at - behind
+
+        def job(i, inner):
+            home = i == 0
+            c = jnp.where(home, own_c, away_c)
+
+            @pl.when((home & jnp.logical_not(late)) | ((i == 1) & (c >= early)))
             def _():
                 halos_here(c)
 
-            for i in range(1, n_tw):
-                q_copy(c, i, source(i)).wait_recv()
-
-            def one(i, inner):
-                attend(c, peer(i))
-                return inner
-
-            lax.fori_loop(1, n_tw, one, 0)
-            for i in range(1, n_tw):
+            @pl.when(jnp.logical_not(home))
+            def _():
+                q_copy(c, n_tw - i, peer(i)).wait_recv()
+
+            attend(c, peer(i))
+
+            @pl.when(home)
+            def _():
+                out_local(c).start()
+
+            @pl.when(jnp.logical_not(home))
+            def _():
                 out_copy(c, i, tw).start()
 
-        @pl.when(((at >= lag) & (at < chunks)) | (at >= 2 * chunks))
-        def _():
-            c = jnp.where(at < chunks, at - lag, at - chunks - lag)
-
-            @pl.when(at < chunks)
-            def _():
-                halos_here(c)
-
-            q_local(c).wait()
-            attend(c, tw)
-            out_local(c).start()
-
+            return inner
+
+        lax.fori_loop(jnp.where(own_now, 0, 1), jnp.where(away_now, n_tw, 1), job, 0)
         return carry
 
-    lax.fori_loop(0, 2 * chunks + lag, step, 0)
-
-    for c in range(chunks):
-        for i in range(1, n_tw):
-            kv_copy(c, i, tw).wait_send()
-            q_copy(c, i, tw).wait_send()
-            out_copy(c, i, tw).wait_send()
-            out_copy(c, i, source(i)).wait_recv()
-        out_local(c).wait()
-
-        @pl.when(has_up)
-        def _():
-            halo_up(c, 0).wait_send()
-
-        @pl.when(has_down)
-        def _():
-            halo_down(c, 0).wait_send()
+    lax.fori_loop(0, 2 * chunks + behind - early, step, 0)
+
+    for i in range(1, n_tw):
+        all_of(kvbuf.at[:, tw, :, own, :], kv_send.at[i - 1])
+        all_of(qbuf.at[:, tw], q_send.at[i - 1])
+        all_of(obuf.at[:, tw], out_send.at[i - 1])
+    all_of(obuf.at[:, tw], loc_sem.at[2])
+
+    @pl.when(has_up)
+    def _():
+        all_of(packed.at[:, :, :, pl.ds(0, halo), :], halo_send.at[0])
+
+    @pl.when(has_down)
+    def _():
+        all_of(packed.at[:, :, :, pl.ds(halo, halo), :], halo_send.at[1])
+
+    for i in range(1, n_tw):
+        all_of(obuf.at[:, tw], out_recv.at[i - 1])
 
 
 def body(sizes, queries, video_kv, text_kv, time_embed, gate_weight, window_extent, tile_valid):
@@ -425,14 +435,16 @@
             pltpu.VMEM((chunks, 1, lanes), jnp.float32),
             pltpu.VMEM((n_tw, tokens, wide * span), jnp.int32),
             pltpu.VMEM((n_tw, tokens, wide * span), jnp.int32),
-            dma((8,)),
-            dma((chunks, 3)),
-            dma((chunks, others, 2)),
-            dma((chunks, others, 2)),
-            dma((chunks, 2)),
-            dma((chunks, 2)),
+            dma((3,)),
+            dma((3,)),
+            dma((others,)),
+            dma((others,)),
             dma((chunks, others)),
             dma((chunks, others)),
+            dma((2,)),
+            dma((chunks, 2)),
+            dma((others,)),
+            dma((others,)),
         ],
         compiler_params=pltpu.CompilerParams(
             collective_id=0, has_side_effects=True, vmem_limit_bytes=56 * 1024 * 1024

time: 31.8 us -> 30.6 us (0.962); the launches traced: 31.2 us -> 30.5 us
  Pallas kernels: 30.4 us -> 29.7 us
    pallas_call x1, Pallas kernels: 30.4 us -> 29.7 us  [body(): pl.pallas_call(functools.partial(kernel, (n_th, n_tw, chunks, lanes, toke...]
where the time goes in v3:
time: 30.6 us; the launch traced here: 30.5 us
  Pallas kernels  29.7 us (97%)
  local copies, waits for them, and re-layouts  0.82 us (3%)
    pallas_call x1, Pallas kernels, body(): pl.pallas_call(functools.partial(kernel, (n_th, n_tw, chunks, lanes, toke...  29.7 us
    unnamed x1, local copies, waits for them, and re-layouts  0.82 us

profile of v3, /device:TPU:1, one launch (start us, length us, event | category | flops | bytes accessed | tf_op | source)
XLA Modules:
  0.0 30.5 jit_solution(243961084210093325)
XLA Ops:
  0.0 29.7 %shard_map.100 = bf16[96,3072]{1,0:T(8,128)(2,1)S(1)} custom-call(s32[2,48]{1,0:T(2,128)} %bitcast.18, s32[2,2,4]{2,1,0:T(2,128)} %bitcast.17, bf16[96,3072]{1,0:T(8,128)(2,1)} %bitcast.16, bf16[2,96,3072]{2,1,0:T(8,128)(2,1)} %bitcast.15, bf16[226,2,1536]{2,1,0:T(2,128)(2,1)} %bitcast.14, bf16[4,128]{1,0:T(4,128)(2,1)} %bitcast.19, ...), custom_call_target="tpu_custom_call" | custom-call | tf_op jit(solution)/shard_map/pallas_call | solution.py:416
  29.7 0.8 %copy.12 = bf16[4,8,3,3072]{3,1,2,0:T(8,128)(2,1)} copy(bf16[4,8,3,3072]{3,1,2,0:T(8,128)(2,1)S(1)} %bitcast.13) | data formatting | bytes 1179648

commit v4 on v3

--- a/solution.py
+++ b/solution.py
@@ -56,15 +56,11 @@
     gate,
     row_gap,
     col_gap,
-    pre_sem,
-    loc_sem,
-    kv_send,
-    q_send,
+    load_sem,
+    done_sem,
     kv_recv,
     q_recv,
-    halo_send,
     halo_recv,
-    out_send,
     out_recv,
 ):
     n_th, n_tw, chunks, lanes, tokens, halo, tile_cols, wide, flat = dims
@@ -92,37 +88,37 @@
 
     def kv_copy(c, i, slot):
         return remote(
-            piece(kv_in, peer(i), c), kvbuf.at[c, slot, :, own, :], kv_send.at[i - 1], kv_recv.at[c, i - 1], {"tw": peer(i)}
+            piece(kv_in, peer(i), c), kvbuf.at[c, slot, :, own, :], done_sem.at[0], kv_recv.at[c, i - 1], {"tw": peer(i)}
         )
 
     def q_copy(c, i, slot):
         return remote(
-            piece(q_in, peer(i), c), qbuf.at[c, slot], q_send.at[i - 1], q_recv.at[c, i - 1], {"tw": peer(i)}
+            piece(q_in, peer(i), c), qbuf.at[c, slot], done_sem.at[0], q_recv.at[c, i - 1], {"tw": peer(i)}
         )
 
     def kv_local(c):
-        return pltpu.make_async_copy(piece(kv_in, tw, c), kvbuf.at[c, tw, :, own, :], loc_sem.at[0])
+        return pltpu.make_async_copy(piece(kv_in, tw, c), kvbuf.at[c, tw, :, own, :], load_sem.at[1])
 
     def q_local(c):
-        return pltpu.make_async_copy(piece(q_in, tw, c), qbuf.at[c, tw], loc_sem.at[1])
-
-    def halo_up(c, landing):
+        return pltpu.make_async_copy(piece(q_in, tw, c), qbuf.at[c, tw], load_sem.at[1])
+
+    def halo_up(c):
         dst = pl.ds(halo + tokens, halo)
         return remote(
-            packed.at[c, :, :, pl.ds(0, halo), :], kvbuf.at[c, :, :, dst, :], halo_send.at[0], halo_recv.at[c, 0], {"th": th - 1 + landing}
-        )
-
-    def halo_down(c, landing):
+            packed.at[c, :, :, pl.ds(0, halo), :], kvbuf.at[c, :, :, dst, :], done_sem.at[0], halo_recv.at[c], {"th": th - 1}
+        )
+
+    def halo_down(c):
         dst = pl.ds(0, halo)
         return remote(
-            packed.at[c, :, :, pl.ds(halo, halo), :], kvbuf.at[c, :, :, dst, :], halo_send.at[1], halo_recv.at[c, 1], {"th": th + 1 - landing}
+            packed.at[c, :, :, pl.ds(halo, halo), :], kvbuf.at[c, :, :, dst, :], done_sem.at[0], halo_recv.at[c], {"th": th + 1}
         )
 
     def out_copy(c, i, slot):
-        return remote(obuf.at[c, peer(i)], piece(out_ref, slot, c), out_send.at[i - 1], out_recv.at[i - 1], {"tw": peer(i)})
+        return remote(obuf.at[c, peer(i)], piece(out_ref, slot, c), done_sem.at[0], out_recv.at[i - 1], {"tw": peer(i)})
 
     def out_local(c):
-        return pltpu.make_async_copy(obuf.at[c, tw], piece(out_ref, tw, c), loc_sem.at[2])
+        return pltpu.make_async_copy(obuf.at[c, tw], piece(out_ref, tw, c), done_sem.at[0])
 
     has_up = th > 0
     has_down = th < n_th - 1
@@ -141,7 +137,7 @@
 
     pl.semaphore_wait(barrier, n_tw - 1 + has_up.astype(jnp.int32) + has_down.astype(jnp.int32))
 
-    behind = chunks // 2
+    behind = max(chunks - 2, 0)
     for c in range(chunks + behind):
         for i in range(1, n_tw):
             if c < chunks:
@@ -149,13 +145,13 @@
             if c >= behind:
                 q_copy(c - behind, i, tw).start()
 
-    gw_load = pltpu.make_async_copy(gw_in, gw_ref, pre_sem.at[0])
-    text_load = pltpu.make_async_copy(text_in, text_raw, pre_sem.at[1])
+    gw_load = pltpu.make_async_copy(gw_in, gw_ref, load_sem.at[0])
+    text_load = pltpu.make_async_copy(text_in, text_raw, load_sem.at[1])
     for c in range(chunks):
         kv_local(c).start()
         q_local(c).start()
     small = [
-        pltpu.make_async_copy(src, dst, pre_sem.at[2])
+        pltpu.make_async_copy(src, dst, load_sem.at[0])
         for src, dst in (
             [
                 (ext_in, ext_ref),
@@ -183,7 +179,6 @@
     def find_gate():
         time = time_ref[...].astype(jnp.float32)
         mod_in = (time / (1.0 + jnp.exp(-time))).astype(jnp.bfloat16)
-        gw_load.wait()
         depth = mod_in.shape[1]
         gate_vec = jnp.zeros((1, chunks * lanes), jnp.float32)
         for k in range(mod_in.shape[0]):
@@ -196,6 +191,7 @@
 
     for load in small:
         load.wait()
+    gw_load.wait()
 
     reach = -(-HALO // tile_cols)
 
@@ -282,16 +278,16 @@
         pltpu.make_async_copy(ref, ref, sem).wait()
 
     def halos_here(c):
-        @pl.when(has_down)
+        @pl.when(has_down & has_up)
         def _():
-            halo_up(c, 2).wait_recv()
-
-        @pl.when(has_up)
+            all_of(packed.at[c], halo_recv.at[c])
+
+        @pl.when(has_down != has_up)
         def _():
-            halo_down(c, 2).wait_recv()
-
-    all_of(kvbuf.at[:, tw, :, own, :], loc_sem.at[0])
-    all_of(qbuf.at[:, tw], loc_sem.at[1])
+            all_of(packed.at[c, :, :, pl.ds(0, halo), :], halo_recv.at[c])
+
+    all_of(kvbuf.at[:, tw, :, own, :], load_sem.at[1])
+    all_of(qbuf.at[:, tw], load_sem.at[1])
 
     def step(at, carry):
         @pl.when(at < chunks)
@@ -309,11 +305,11 @@
 
             @pl.when(has_up)
             def _():
-                halo_up(at, 0).start()
+                halo_up(at).start()
 
             @pl.when(has_down)
             def _():
-                halo_down(at, 0).start()
+                halo_down(at).start()
 
             mine = slice(None) if chunks == 1 else pl.ds(pl.multiple_of(at * lanes, lanes), lanes)
             for s in range(2):
@@ -355,18 +351,18 @@
     lax.fori_loop(0, 2 * chunks + behind - early, step, 0)
 
     for i in range(1, n_tw):
-        all_of(kvbuf.at[:, tw, :, own, :], kv_send.at[i - 1])
-        all_of(qbuf.at[:, tw], q_send.at[i - 1])
-        all_of(obuf.at[:, tw], out_send.at[i - 1])
-    all_of(obuf.at[:, tw], loc_sem.at[2])
+        all_of(kvbuf.at[:, tw, :, own, :], done_sem.at[0])
+        all_of(qbuf.at[:, tw], done_sem.at[0])
+        all_of(obuf.at[:, tw], done_sem.at[0])
+    all_of(obuf.at[:, tw], done_sem.at[0])
 
     @pl.when(has_up)
     def _():
-        all_of(packed.at[:, :, :, pl.ds(0, halo), :], halo_send.at[0])
+        all_of(packed.at[:, :, :, pl.ds(0, halo), :], done_sem.at[0])
 
     @pl.when(has_down)
     def _():
-        all_of(packed.at[:, :, :, pl.ds(halo, halo), :], halo_send.at[1])
+        all_of(packed.at[:, :, :, pl.ds(halo, halo), :], done_sem.at[0])
 
     for i in range(1, n_tw):
         all_of(obuf.at[:, tw], out_recv.at[i - 1])
@@ -435,15 +431,11 @@
             pltpu.VMEM((chunks, 1, lanes), jnp.float32),
             pltpu.VMEM((n_tw, tokens, wide * span), jnp.int32),
             pltpu.VMEM((n_tw, tokens, wide * span), jnp.int32),
-            dma((3,)),
-            dma((3,)),
-            dma((others,)),
-            dma((others,)),
+            dma((2,)),
+            dma((1,)),
             dma((chunks, others)),
             dma((chunks, others)),
-            dma((2,)),
-            dma((chunks, 2)),
-            dma((others,)),
+            dma((chunks,)),
             dma((others,)),
         ],
         compiler_params=pltpu.CompilerParams(

time: 30.6 us -> 30.5 us (level)
  no operation moved by 1% of the time
where the time goes in v4:
time: 30.5 us; the launch traced here: 30.4 us
  Pallas kernels  29.5 us (97%)
  local copies, waits for them, and re-layouts  0.82 us (3%)
    pallas_call x1, Pallas kernels, body(): pl.pallas_call(functools.partial(kernel, (n_th, n_tw, chunks, lanes, toke...  29.5 us
    unnamed x1, local copies, waits for them, and re-layouts  0.82 us

profile of v4, /device:TPU:1, one launch (start us, length us, event | category | flops | bytes accessed | tf_op | source)
XLA Modules:
  0.0 30.4 jit_solution(1052900372309734200)
XLA Ops:
  0.0 29.5 %shard_map.100 = bf16[96,3072]{1,0:T(8,128)(2,1)S(1)} custom-call(s32[2,48]{1,0:T(2,128)} %bitcast.18, s32[2,2,4]{2,1,0:T(2,128)} %bitcast.17, bf16[96,3072]{1,0:T(8,128)(2,1)} %bitcast.16, bf16[2,96,3072]{2,1,0:T(8,128)(2,1)} %bitcast.15, bf16[226,2,1536]{2,1,0:T(2,128)(2,1)} %bitcast.14, bf16[4,128]{1,0:T(4,128)(2,1)} %bitcast.19, ...), custom_call_target="tpu_custom_call" | custom-call | tf_op jit(solution)/shard_map/pallas_call | solution.py:412
  29.6 0.8 %copy.12 = bf16[4,8,3,3072]{3,1,2,0:T(8,128)(2,1)} copy(bf16[4,8,3,3072]{3,1,2,0:T(8,128)(2,1)S(1)} %bitcast.13) | data formatting | bytes 1179648

commit v5 on v4

--- a/solution.py
+++ b/solution.py
@@ -54,14 +54,15 @@
     text_ref,
     gw_ref,
     gate,
-    row_gap,
-    col_gap,
+    window,
     load_sem,
     done_sem,
     kv_recv,
     q_recv,
     halo_recv,
     out_recv,
+    held,
+    held_recv,
 ):
     n_th, n_tw, chunks, lanes, tokens, halo, tile_cols, wide, flat = dims
     span = tokens + 2 * halo
@@ -117,6 +118,14 @@
     def out_copy(c, i, slot):
         return remote(obuf.at[c, peer(i)], piece(out_ref, slot, c), done_sem.at[0], out_recv.at[i - 1], {"tw": peer(i)})
 
+    def detour_copy():
+        return remote(
+            piece(q_in, peer(1), astray), held, done_sem.at[0], held_recv.at[0], {"th": turn, "tw": peer(1)}
+        )
+
+    def detour_last():
+        return remote(held, qbuf.at[astray, peer(1)], done_sem.at[0], q_recv.at[astray, 0], {"th": 0})
+
     def out_local(c):
         return pltpu.make_async_copy(obuf.at[c, tw], piece(out_ref, tw, c), done_sem.at[0])
 
@@ -138,12 +147,23 @@
     pl.semaphore_wait(barrier, n_tw - 1 + has_up.astype(jnp.int32) + has_down.astype(jnp.int32))
 
     behind = max(chunks - 2, 0)
+    lag = min(2, chunks)
+    early = max(0, chunks - 1 - lag)
+    detour = n_tw == 2 and n_th >= 4 and early > 2 and chunks > behind + 1
+    turn = n_th // 2
+    astray = chunks - 1 - behind
     for c in range(chunks + behind):
         for i in range(1, n_tw):
             if c < chunks:
                 kv_copy(c, i, tw).start()
-            if c >= behind:
+            if c >= behind and not (detour and c - behind == astray):
                 q_copy(c - behind, i, tw).start()
+        if detour and c - behind == astray:
+
+            @pl.when(th != 0)
+            def _():
+                q_copy(astray, 1, tw).start()
+
 
     gw_load = pltpu.make_async_copy(gw_in, gw_ref, load_sem.at[0])
     text_load = pltpu.make_async_copy(text_in, text_raw, load_sem.at[1])
@@ -207,7 +227,7 @@
     above = jnp.maximum(th - 1, 0)
     below = jnp.minimum(th + 1, n_th - 1)
 
-    def distances(t, carry):
+    def windows(t, carry):
         start = first_tile(t)
         for j in range(wide):
             tc = start + j
@@ -218,28 +238,41 @@
                 down = jnp.where(has_down, valid_ref[tc, what, below], 0)
                 limits.append(jnp.where(k_band == 0, up, jnp.where(k_band == 1, mid, down)))
             bad = jnp.where((k_local < limits[0]) & (k_col < limits[1]), 0, FAR)
-            row_gap[t, :, pl.ds(j * span, span)] = jnp.abs(k_row - q_row) + bad
-            col_gap[t, :, pl.ds(j * span, span)] = jnp.abs(k_col + (tc - t) * tile_cols - q_col)
+            row_gap = jnp.abs(k_row - q_row) + bad
+            col_gap = jnp.abs(k_col + (tc - t) * tile_cols - q_col)
+            for r in range(HALO):
+                near = row_gap <= r + 1
+                for k in range(HALO):
+                    window[t, r * HALO + k, :, pl.ds(j * span, span)] = jnp.where(near & (col_gap <= k + 1), 0.0, NEG)
         return carry
 
-    lax.fori_loop(0, n_tw, distances, 0)
+    lax.fori_loop(0, n_tw, windows, 0)
     find_gate()
     text_load.wait()
+    texts = text_raw.shape[0]
+    padded = text_ref.shape[2]
+    if padded > texts:
+        text_ref[:, :, texts // 16 * 16 :, :] = jnp.zeros((chunks, 2, padded - texts // 16 * 16, lanes), text_ref.dtype)
+
+    video = wide * span
+    beyond = texts // GROUP * GROUP
 
     def attend(c, t):
         start = first_tile(t)
         q_ok = (q_row < valid_ref[t, 0, th]) & (q_col < valid_ref[t, 1, th])
-        rows_apart = row_gap[t]
-        cols_apart = col_gap[t]
+        tail = lax.broadcasted_iota(jnp.int32, (1, padded - beyond), 1) + beyond
+        tail_bias = jnp.where(tail < texts, 0.0, NEG)
         for low in range(0, lanes, GROUP):
             width = min(GROUP, lanes - low)
             count = width // HEAD_DIM
             part = pl.ds(low, width)
             q = qbuf[c, t, :, part]
-            keys = kvbuf[c, pl.ds(start, wide), 0, :, part].reshape(wide * span, width)
-            values = kvbuf[c, pl.ds(start, wide), 1, :, part].reshape(wide * span, width)
-            t_keys = text_ref[c, 0, :, part]
-            t_values = text_ref[c, 1, :, part]
+            keys, values = [
+                jnp.concatenate(
+                    [kvbuf[c, pl.ds(start, wide), s, :, part].reshape(video, width), text_ref[c, s, :, part]], axis=0
+                )
+                for s in range(2)
+            ]
             lane = lax.broadcasted_iota(jnp.int32, (1, width), 1)
             stacked = []
             for s in range(count):
@@ -247,33 +280,29 @@
                 stacked.append(q * jnp.where(mine, HEAD_DIM ** -0.5, 0.0).astype(jnp.bfloat16))
             q_all = jnp.concatenate(stacked, axis=0) if count > 1 else stacked[0]
             scores = dot_nt(q_all, keys)
-            t_scores = dot_nt(q_all, t_keys)
-            weights, t_weights, inverse = [], [], []
+            weights, inverse = [], []
             for s in range(count):
                 head = tw * (chunks * heads_per_chunk) + c * heads_per_chunk + low // HEAD_DIM + s
-                allowed = (rows_apart <= ext_ref[0, head]) & (cols_apart <= ext_ref[1, head])
-                sv = jnp.where(allowed, scores[s * tokens : (s + 1) * tokens], NEG)
-                st = t_scores[s * tokens : (s + 1) * tokens]
-                top = jnp.maximum(jnp.max(sv, axis=-1, keepdims=True), jnp.max(st, axis=-1, keepdims=True))
-                ev = jnp.exp(sv - top)
-                et = jnp.exp(st - top)
-                inverse.append(1.0 / (jnp.sum(ev, axis=-1, keepdims=True) + jnp.sum(et, axis=-1, keepdims=True)))
-                weights.append(ev.astype(jnp.bfloat16))
-                t_weights.append(et.astype(jnp.bfloat16))
+                reach_at = (jnp.clip(ext_ref[0, head], 1, HALO) - 1) * HALO + jnp.clip(ext_ref[1, head], 1, HALO) - 1
+                mine = scores[s * tokens : (s + 1) * tokens]
+                pieces = [mine[:, :video] + window[t, reach_at]]
+                if beyond:
+                    pieces.append(mine[:, video : video + beyond])
+                if padded > beyond:
+                    pieces.append(mine[:, video + beyond :] + tail_bias)
+                near = jnp.concatenate(pieces, axis=1)
+                top = jnp.max(near, axis=-1, keepdims=True)
+                e = jnp.exp(near - top)
+                inverse.append(1.0 / jnp.sum(e, axis=-1, keepdims=True))
+                weights.append(e.astype(jnp.bfloat16))
             w_all = jnp.concatenate(weights, axis=0) if count > 1 else weights[0]
-            tw_all = jnp.concatenate(t_weights, axis=0) if count > 1 else t_weights[0]
-            mixed = jnp.dot(w_all, values, preferred_element_type=jnp.float32) + jnp.dot(
-                tw_all, t_values, preferred_element_type=jnp.float32
-            )
+            mixed = jnp.dot(w_all, values, preferred_element_type=jnp.float32)
             result = mixed[0:tokens] * inverse[0]
             for s in range(1, count):
                 result = jnp.where(lane >= s * HEAD_DIM, mixed[s * tokens : (s + 1) * tokens] * inverse[s], result)
             result = result * gate[c, :, part]
             obuf[c, t, :, part] = jnp.where(q_ok, result, 0.0).astype(jnp.bfloat16)
 
-    lag = min(2, chunks)
-    early = max(0, chunks - 1 - lag)
-
     def all_of(ref, sem):
         pltpu.make_async_copy(ref, ref, sem).wait()
 
@@ -290,6 +319,13 @@
     all_of(qbuf.at[:, tw], load_sem.at[1])
 
     def step(at, carry):
+        if detour:
+
+            @pl.when((th == turn) & (at == lag + early - 1))
+            def _():
+                all_of(held, held_recv.at[0])
+                detour_last().start()
+
         @pl.when(at < chunks)
         def _():
             for i in range(1, n_tw):
@@ -311,9 +347,23 @@
             def _():
                 halo_down(at).start()
 
-            mine = slice(None) if chunks == 1 else pl.ds(pl.multiple_of(at * lanes, lanes), lanes)
-            for s in range(2):
-                text_ref[at, s] = text_raw[:, s, mine]
+        @pl.when((at >= lag) & (at < lag + early))
+        def _():
+            halos_here(at - lag)
+
+        if detour:
+
+            @pl.when((th == 0) & (at == lag))
+            def _():
+                detour_copy().start()
+
+        @pl.when(at < -(-chunks // 2))
+        def _():
+            for k in range(min(2, chunks)):
+                c = jnp.minimum(2 * at + k, chunks - 1)
+                mine = slice(None) if chunks == 1 else pl.ds(pl.multiple_of(c * lanes, lanes), lanes)
+                for s in range(2):
+                    text_ref[c, s, :texts] = text_raw[:, s, mine]
 
         late = at >= chunks + behind
         own_now = ((at >= lag) & (at < lag + early)) | late
@@ -325,7 +375,7 @@
             home = i == 0
             c = jnp.where(home, own_c, away_c)
 
-            @pl.when((home & jnp.logical_not(late)) | ((i == 1) & (c >= early)))
+            @pl.when((i == 1) & (c >= early))
             def _():
                 halos_here(c)
 
@@ -355,6 +405,12 @@
         all_of(qbuf.at[:, tw], done_sem.at[0])
         all_of(obuf.at[:, tw], done_sem.at[0])
     all_of(obuf.at[:, tw], done_sem.at[0])
+
+    if detour:
+
+        @pl.when(th == turn)
+        def _():
+            all_of(held, done_sem.at[0])
 
     @pl.when(has_up)
     def _():
@@ -426,17 +482,18 @@
             pltpu.VMEM((chunks, n_tw, 2, 2 * halo, lanes), jnp.bfloat16),
             pltpu.VMEM((chunks, n_tw, tokens, lanes), jnp.bfloat16),
             pltpu.VMEM((text_kv.shape[1], 2, text_kv.shape[2]), jnp.bfloat16),
-            pltpu.VMEM((chunks, 2, text_kv.shape[1], lanes), jnp.bfloat16),
+            pltpu.VMEM((chunks, 2, -(-text_kv.shape[1] // GROUP) * GROUP, lanes), jnp.bfloat16),
             pltpu.VMEM(gate_weight.shape, jnp.bfloat16),
             pltpu.VMEM((chunks, 1, lanes), jnp.float32),
-            pltpu.VMEM((n_tw, tokens, wide * span), jnp.int32),
-            pltpu.VMEM((n_tw, tokens, wide * span), jnp.int32),
+            pltpu.VMEM((n_tw, HALO * HALO, tokens, wide * span), jnp.float32),
             dma((2,)),
             dma((1,)),
             dma((chunks, others)),
             dma((chunks, others)),
             dma((chunks,)),
             dma((others,)),
+            pltpu.VMEM((tokens, lanes), jnp.bfloat16),
+            dma((1,)),
         ],
         compiler_params=pltpu.CompilerParams(
             collective_id=0, has_side_effects=True, vmem_limit_bytes=56 * 1024 * 1024

time: 30.5 us -> 30.1 us (0.987)
  Pallas kernels: 29.5 us -> 29 us
    pallas_call x1, Pallas kernels: 29.5 us -> 29 us  [body(): pl.pallas_call(functools.partial(kernel, (n_th, n_tw, chunks, lanes, toke...]
where the time goes in v5:
time: 30.1 us; the launch traced here: 29.9 us
  Pallas kernels  29 us (96%)
  local copies, waits for them, and re-layouts  0.82 us (3%)
    pallas_call x1, Pallas kernels, body(): pl.pallas_call(functools.partial(kernel, (n_th, n_tw, chunks, lanes, toke...  29 us
    unnamed x1, local copies, waits for them, and re-layouts  0.82 us

profile of v5, /device:TPU:1, one launch (start us, length us, event | category | flops | bytes accessed | tf_op | source)
XLA Modules:
  0.0 29.9 jit_solution(15275342629713156799)
XLA Ops:
  0.0 29.0 %shard_map.100 = bf16[96,3072]{1,0:T(8,128)(2,1)S(1)} custom-call(s32[2,48]{1,0:T(2,128)} %bitcast.18, s32[2,2,4]{2,1,0:T(2,128)} %bitcast.17, bf16[96,3072]{1,0:T(8,128)(2,1)} %bitcast.16, bf16[2,96,3072]{2,1,0:T(8,128)(2,1)} %bitcast.15, bf16[226,2,1536]{2,1,0:T(2,128)(2,1)} %bitcast.14, bf16[4,128]{1,0:T(4,128)(2,1)} %bitcast.19, ...), custom_call_target="tpu_custom_call" | custom-call | tf_op jit(solution)/shard_map/pallas_call | solution.py:468
  29.0 0.8 %copy.12 = bf16[4,8,3,3072]{3,1,2,0:T(8,128)(2,1)} copy(bf16[4,8,3,3072]{3,1,2,0:T(8,128)(2,1)S(1)} %bitcast.13) | data formatting | bytes 1179648

commit v6 on v5

--- a/solution.py
+++ b/solution.py
@@ -150,7 +150,7 @@
     lag = min(2, chunks)
     early = max(0, chunks - 1 - lag)
     detour = n_tw == 2 and n_th >= 4 and early > 2 and chunks > behind + 1
-    turn = n_th // 2
+    turn = 2
     astray = chunks - 1 - behind
     for c in range(chunks + behind):
         for i in range(1, n_tw):
@@ -163,7 +163,6 @@
             @pl.when(th != 0)
             def _():
                 q_copy(astray, 1, tw).start()
-
 
     gw_load = pltpu.make_async_copy(gw_in, gw_ref, load_sem.at[0])
     text_load = pltpu.make_async_copy(text_in, text_raw, load_sem.at[1])

time: 30.1 us -> 30.1 us (level)
  no operation moved by 1% of the time
where the time goes in v6:
time: 30.1 us; the launch traced here: 29.9 us
  Pallas kernels  29 us (96%)
  local copies, waits for them, and re-layouts  0.82 us (3%)
    pallas_call x1, Pallas kernels, body(): pl.pallas_call(functools.partial(kernel, (n_th, n_tw, chunks, lanes, toke...  29 us
    unnamed x1, local copies, waits for them, and re-layouts  0.82 us

profile of v6, /device:TPU:1, one launch (start us, length us, event | category | flops | bytes accessed | tf_op | source)
XLA Modules:
  0.0 29.9 jit_solution(15275342629713156799)
XLA Ops:
  0.0 29.0 %shard_map.100 = bf16[96,3072]{1,0:T(8,128)(2,1)S(1)} custom-call(s32[2,48]{1,0:T(2,128)} %bitcast.18, s32[2,2,4]{2,1,0:T(2,128)} %bitcast.17, bf16[96,3072]{1,0:T(8,128)(2,1)} %bitcast.16, bf16[2,96,3072]{2,1,0:T(8,128)(2,1)} %bitcast.15, bf16[226,2,1536]{2,1,0:T(2,128)(2,1)} %bitcast.14, bf16[4,128]{1,0:T(4,128)(2,1)} %bitcast.19, ...), custom_call_target="tpu_custom_call" | custom-call | tf_op jit(solution)/shard_map/pallas_call | solution.py:467
  29.0 0.8 %copy.12 = bf16[4,8,3,3072]{3,1,2,0:T(8,128)(2,1)} copy(bf16[4,8,3,3072]{3,1,2,0:T(8,128)(2,1)S(1)} %bitcast.13) | data formatting | bytes 1179648

commit v7 on v4

v7 whole, which is shorter than its diff:
```python
import functools

import jax
import jax.numpy as jnp
import numpy as np
from jax import lax
from jax.experimental import pallas as pl
from jax.experimental.pallas import tpu as pltpu
from jax.sharding import PartitionSpec as P

HEAD_DIM = 64
HALO = 3
NEG = -1e30
FAR = 1 << 20
GROUP = 128
MESH = pl.DeviceIdType.MESH


def halo_rows(tile_rows, per_row):
    for rows in range(HALO, tile_rows + 1):
        if rows * per_row % 16 == 0:
            return rows
    return tile_rows


def dot_nt(a, b):
    return lax.dot_general(a, b, (((1,), (1,)), ((), ())), preferred_element_type=jnp.float32)


def kernel(
    dims,
    ext_in,
    valid_in,
    q_in,
    kv_in,
    text_in,
    time_in,
    gw_in,
    qmeta_in,
    kmeta_in,
    perm_in,
    out_ref,
    ext_ref,
    valid_ref,
    time_ref,
    qmeta,
    kmeta,
    perm,
    qbuf,
    kvbuf,
    packed,
    obuf,
    text_raw,
    text_ref,
    gw_ref,
    gate,
    window,
    done_sem,
    out_recv,
    held,
):
    n_th, n_tw, chunks, lanes, tokens, halo, tile_cols, wide, flat = dims
    th = lax.axis_index("th")
    tw = lax.axis_index("tw")
    own = pl.ds(halo, tokens)
    has_up = th > 0
    has_down = th < n_th - 1
    others = max(n_tw - 1, 1)
    dma = pltpu.SemaphoreType.DMA

    def all_of(ref, sem):
        pltpu.make_async_copy(ref, ref, sem).wait()

    behind = max(chunks - 2, 0)
    lag = min(2, chunks)
    early = max(0, chunks - 1 - lag)
    detour = n_tw == 2 and n_th >= 4 and early > 2 and chunks > behind + 1
    turn = 2
    astray = chunks - 1 - behind

    def gather_and_attend(load_sem, kv_recv, q_recv, halo_recv, held_recv):
        span = tokens + 2 * halo
        heads_per_chunk = lanes // HEAD_DIM

        def peer(i):
            return lax.rem(tw + i, n_tw)

        def source(i):
            return lax.rem(tw + n_tw - i, n_tw)

        def piece(ref, j, c):
            if flat:
                return ref.at[..., pl.ds(pl.multiple_of((j * chunks + c) * lanes, lanes), lanes)]
            return ref.at[j, c]

        def remote(src, dst, ssem, rsem, where):
            return pltpu.make_async_remote_copy(
                src_ref=src, dst_ref=dst, send_sem=ssem, recv_sem=rsem, device_id=where, device_id_type=MESH
            )

        def kv_copy(c, i, slot):
            return remote(
                piece(kv_in, peer(i), c), kvbuf.at[c, slot, :, own, :], done_sem.at[0], kv_recv.at[c, i - 1], {"tw": peer(i)}
            )

        def q_copy(c, i, slot):
            return remote(
                piece(q_in, peer(i), c), qbuf.at[c, slot], done_sem.at[0], q_recv.at[c, i - 1], {"tw": peer(i)}
            )

        def kv_local(c):
            return pltpu.make_async_copy(piece(kv_in, tw, c), kvbuf.at[c, tw, :, own, :], load_sem.at[1])

        def q_local(c):
            return pltpu.make_async_copy(piece(q_in, tw, c), qbuf.at[c, tw], load_sem.at[1])

        def halo_up(c):
            dst = pl.ds(halo + tokens, halo)
            return remote(
                packed.at[c, :, :, pl.ds(0, halo), :], kvbuf.at[c, :, :, dst, :], done_sem.at[0], halo_recv.at[c], {"th": th - 1}
            )

        def halo_down(c):
            dst = pl.ds(0, halo)
            return remote(
                packed.at[c, :, :, pl.ds(halo, halo), :], kvbuf.at[c, :, :, dst, :], done_sem.at[0], halo_recv.at[c], {"th": th + 1}
            )

        def out_copy(c, i, slot):
            return remote(obuf.at[c, peer(i)], piece(out_ref, slot, c), done_sem.at[0], out_recv.at[i - 1], {"tw": peer(i)})

        def detour_copy():
            return remote(
                piece(q_in, peer(1), astray), held, done_sem.at[0], held_recv.at[0], {"th": turn, "tw": peer(1)}
            )

        def detour_last():
            return remote(held, qbuf.at[astray, peer(1)], done_sem.at[0], q_recv.at[astray, 0], {"th": 0})

        def out_local(c):
            return pltpu.make_async_copy(obuf.at[c, tw], piece(out_ref, tw, c), done_sem.at[0])

        barrier = pltpu.get_barrier_semaphore()
        for i in range(1, n_tw):
            pl.semaphore_signal(barrier, inc=1, device_id={"tw": peer(i)}, device_id_type=MESH)

        @pl.when(has_up)
        def _():
            pl.semaphore_signal(barrier, inc=1, device_id={"th": th - 1}, device_id_type=MESH)

        @pl.when(has_down)
        def _():
            pl.semaphore_signal(barrier, inc=1, device_id={"th": th + 1}, device_id_type=MESH)

        pl.semaphore_wait(barrier, n_tw - 1 + has_up.astype(jnp.int32) + has_down.astype(jnp.int32))

        for c in range(chunks + behind):
            for i in range(1, n_tw):
                if c < chunks:
                    kv_copy(c, i, tw).start()
                if c >= behind and not (detour and c - behind == astray):
                    q_copy(c - behind, i, tw).start()
            if detour and c - behind == astray:

                @pl.when(th != 0)
                def _():
                    q_copy(astray, 1, tw).start()

        gw_load = pltpu.make_async_copy(gw_in, gw_ref, load_sem.at[0])
        text_load = pltpu.make_async_copy(text_in, text_raw, load_sem.at[1])
        for c in range(chunks):
            kv_local(c).start()
            q_local(c).start()
        small = [
            pltpu.make_async_copy(src, dst, load_sem.at[0])
            for src, dst in (
                [
                    (ext_in, ext_ref),
                    (valid_in, valid_ref),
                    (time_in, time_ref),
                    (qmeta_in, qmeta),
                    (kmeta_in, kmeta),
                    (perm_in, perm),
                ]
            )
        ]
        for load in small:
            load.start()
        gw_load.start()
        text_load.start()

        @pl.when(jnp.logical_not(has_up))
        def _():
            kvbuf[:, :, :, pl.ds(0, halo), :] = jnp.zeros((chunks, n_tw, 2, halo, lanes), kvbuf.dtype)

        @pl.when(jnp.logical_not(has_down))
        def _():
            kvbuf[:, :, :, pl.ds(halo + tokens, halo), :] = jnp.zeros((chunks, n_tw, 2, halo, lanes), kvbuf.dtype)

        def find_gate():
            time = time_ref[...].astype(jnp.float32)
            mod_in = (time / (1.0 + jnp.exp(-time))).astype(jnp.bfloat16)
            depth = mod_in.shape[1]
            gate_vec = jnp.zeros((1, chunks * lanes), jnp.float32)
            for k in range(mod_in.shape[0]):
                gate_vec = gate_vec + jnp.dot(
                    mod_in[k : k + 1], gw_ref[k * depth : (k + 1) * depth], preferred_element_type=jnp.float32
                )
            gate_vec = gate_vec.astype(jnp.bfloat16).astype(jnp.float32)
            for c in range(chunks):
                gate[c] = gate_vec[:, c * lanes : (c + 1) * lanes]

        for load in small:
            load.wait()
        gw_load.wait()

        reach = -(-HALO // tile_cols)

        def first_tile(t):
            return jnp.clip(t - reach, 0, n_tw - wide)

        q_row = qmeta[:, 0:1]
        q_col = qmeta[:, 1:2]
        k_row = kmeta[0:1, :]
        k_band = kmeta[1:2, :]
        k_local = kmeta[2:3, :]
        k_col = kmeta[3:4, :]
        above = jnp.maximum(th - 1, 0)
        below = jnp.minimum(th + 1, n_th - 1)

        def windows(t, carry):
            start = first_tile(t)
            for j in range(wide):
                tc = start + j
                limits = []
                for what in range(2):
                    up = jnp.where(has_up, valid_ref[tc, what, above], 0)
                    mid = valid_ref[tc, what, th]
                    down = jnp.where(has_down, valid_ref[tc, what, below], 0)
                    limits.append(jnp.where(k_band == 0, up, jnp.where(k_band == 1, mid, down)))
                bad = jnp.where((k_local < limits[0]) & (k_col < limits[1]), 0, FAR)
                row_gap = jnp.abs(k_row - q_row) + bad
                col_gap = jnp.abs(k_col + (tc - t) * tile_cols - q_col)
                for r in range(HALO):
                    near = row_gap <= r + 1
                    for k in range(HALO):
                        window[t, r * HALO + k, :, pl.ds(j * span, span)] = jnp.where(near & (col_gap <= k + 1), 0.0, NEG)
            return carry

        lax.fori_loop(0, n_tw, windows, 0)
        find_gate()
        text_load.wait()
        texts = text_raw.shape[0]
        padded = text_ref.shape[2]
        if padded > texts:
            text_ref[:, :, texts // 16 * 16 :, :] = jnp.zeros((chunks, 2, padded - texts // 16 * 16, lanes), text_ref.dtype)

        video = wide * span
        beyond = texts // GROUP * GROUP

        def attend(c, t):
            start = first_tile(t)
            q_ok = (q_row < valid_ref[t, 0, th]) & (q_col < valid_ref[t, 1, th])
            tail = lax.broadcasted_iota(jnp.int32, (1, padded - beyond), 1) + beyond
            tail_bias = jnp.where(tail < texts, 0.0, NEG)
            for low in range(0, lanes, GROUP):
                width = min(GROUP, lanes - low)
                count = width // HEAD_DIM
                part = pl.ds(low, width)
                q = qbuf[c, t, :, part]
                keys, values = [
                    jnp.concatenate(
                        [kvbuf[c, pl.ds(start, wide), s, :, part].reshape(video, width), text_ref[c, s, :, part]], axis=0
                    )
                    for s in range(2)
                ]
                lane = lax.broadcasted_iota(jnp.int32, (1, width), 1)
                stacked = []
                for s in range(count):
                    mine = (lane >= s * HEAD_DIM) & (lane < (s + 1) * HEAD_DIM)
                    stacked.append(q * jnp.where(mine, HEAD_DIM ** -0.5, 0.0).astype(jnp.bfloat16))
                q_all = jnp.concatenate(stacked, axis=0) if count > 1 else stacked[0]
                scores = dot_nt(q_all, keys)
                weights, inverse = [], []
                for s in range(count):
                    head = tw * (chunks * heads_per_chunk) + c * heads_per_chunk + low // HEAD_DIM + s
                    reach_at = (jnp.clip(ext_ref[0, head], 1, HALO) - 1) * HALO + jnp.clip(ext_ref[1, head], 1, HALO) - 1
                    mine = scores[s * tokens : (s + 1) * tokens]
                    pieces = [mine[:, :video] + window[t, reach_at]]
                    if beyond:
                        pieces.append(mine[:, video : video + beyond])
                    if padded > beyond:
                        pieces.append(mine[:, video + beyond :] + tail_bias)
                    near = jnp.concatenate(pieces, axis=1)
                    top = jnp.max(near, axis=-1, keepdims=True)
                    e = jnp.exp(near - top)
                    inverse.append(1.0 / jnp.sum(e, axis=-1, keepdims=True))
                    weights.append(e.astype(jnp.bfloat16))
                w_all = jnp.concatenate(weights, axis=0) if count > 1 else weights[0]
                mixed = jnp.dot(w_all, values, preferred_element_type=jnp.float32)
                result = mixed[0:tokens] * inverse[0]
                for s in range(1, count):
                    result = jnp.where(lane >= s * HEAD_DIM, mixed[s * tokens : (s + 1) * tokens] * inverse[s], result)
                result = result * gate[c, :, part]
                obuf[c, t, :, part] = jnp.where(q_ok, result, 0.0).astype(jnp.bfloat16)

        def halos_here(c):
            @pl.when(has_down & has_up)
            def _():
                all_of(packed.at[c], halo_recv.at[c])

            @pl.when(has_down != has_up)
            def _():
                all_of(packed.at[c, :, :, pl.ds(0, halo), :], halo_recv.at[c])

        all_of(kvbuf.at[:, tw, :, own, :], load_sem.at[1])
        all_of(qbuf.at[:, tw], load_sem.at[1])

        def step(at, carry):
            if detour:

                @pl.when((th == turn) & (at == lag + early - 1))
                def _():
                    all_of(held, held_recv.at[0])
                    detour_last().start()

            @pl.when(at < chunks)
            def _():
                for i in range(1, n_tw):
                    kv_copy(at, i, source(i)).wait_recv()

                def pack(j, inner):
                    for s in range(2):
                        rows = jnp.dot(perm[...], kvbuf[at, j, s, own, :], preferred_element_type=jnp.float32)
                        packed[at, j, s] = rows.astype(jnp.bfloat16)
                    return inner

                lax.fori_loop(0, n_tw, pack, 0)

                @pl.when(has_up)
                def _():
                    halo_up(at).start()

                @pl.when(has_down)
                def _():
                    halo_down(at).start()

            @pl.when((at >= lag) & (at < lag + early))
            def _():
                halos_here(at - lag)

            if detour:

                @pl.when((th == 0) & (at == lag))
                def _():
                    detour_copy().start()

            @pl.when(at < -(-chunks // 2))
            def _():
                for k in range(min(2, chunks)):
                    c = jnp.minimum(2 * at + k, chunks - 1)
                    mine = slice(None) if chunks == 1 else pl.ds(pl.multiple_of(c * lanes, lanes), lanes)
                    for s in range(2):
                        text_ref[c, s, :texts] = text_raw[:, s, mine]

            late = at >= chunks + behind
            own_now = ((at >= lag) & (at < lag + early)) | late
            away_now = (at >= behind) & jnp.logical_not(late)
            own_c = jnp.where(late, at - (chunks + behind) + early, at - lag)
            away_c = at - behind

            def job(i, inner):
                home = i == 0
                c = jnp.where(home, own_c, away_c)

                @pl.when((i == 1) & (c >= early))
                def _():
                    halos_here(c)

                @pl.when(jnp.logical_not(home))
                def _():
                    q_copy(c, n_tw - i, peer(i)).wait_recv()

                attend(c, peer(i))

                @pl.when(home)
                def _():
                    out_local(c).start()

                @pl.when(jnp.logical_not(home))
                def _():
                    out_copy(c, i, tw).start()

                return inner

            lax.fori_loop(jnp.where(own_now, 0, 1), jnp.where(away_now, n_tw, 1), job, 0)
            return carry

        lax.fori_loop(0, 2 * chunks + behind - early, step, 0)

    pl.run_scoped(
        gather_and_attend,
        dma((2,)),
        dma((chunks, others)),
        dma((chunks, others)),
        dma((chunks,)),
        dma((1,)),
    )

    for i in range(1, n_tw):
        all_of(kvbuf.at[:, tw, :, own, :], done_sem.at[0])
        all_of(qbuf.at[:, tw], done_sem.at[0])
        all_of(obuf.at[:, tw], done_sem.at[0])
    all_of(obuf.at[:, tw], done_sem.at[0])

    if detour:

        @pl.when(th == turn)
        def _():
            all_of(held, done_sem.at[0])

    @pl.when(has_up)
    def _():
        all_of(packed.at[:, :, :, pl.ds(0, halo), :], done_sem.at[0])

    @pl.when(has_down)
    def _():
        all_of(packed.at[:, :, :, pl.ds(halo, halo), :], done_sem.at[0])

    for i in range(1, n_tw):
        all_of(obuf.at[:, tw], out_recv.at[i - 1])


def body(sizes, queries, video_kv, text_kv, time_embed, gate_weight, window_extent, tile_valid):
    n_th, n_tw = sizes
    frames, tile_rows, tile_cols, model_width = queries.shape
    per_row = frames * tile_cols
    tokens = tile_rows * per_row
    rows = halo_rows(tile_rows, per_row)
    halo = rows * per_row
    span = tokens + 2 * halo
    own_width = model_width // n_tw
    lanes = 2 * GROUP if own_width % (2 * GROUP) == 0 else own_width
    chunks = own_width // lanes
    wide = min(n_tw, 2 * -(-HALO // tile_cols) + 1)

    flat = lanes % GROUP == 0

    q = queries.transpose(0, 2, 1, 3).reshape(tokens, model_width)
    kv = video_kv.transpose(0, 1, 3, 2, 4).reshape(2, tokens, model_width)
    out_form = (tokens, model_width)
    if not flat:
        q = q.reshape(tokens, n_tw, chunks, lanes).transpose(1, 2, 0, 3)
        kv = kv.reshape(2, tokens, n_tw, chunks, lanes).transpose(2, 3, 0, 1, 4)
        out_form = (n_tw, chunks, tokens, lanes)

    ids = np.arange(tokens)
    q_col, q_row = ids // tile_rows % tile_cols, ids % tile_rows
    q_meta = np.stack([q_row, q_col], axis=1).astype(np.int32)
    h_ids = np.arange(halo)
    h_block, h_row = h_ids // rows, h_ids % rows
    k_row = np.concatenate([h_row - rows, q_row, h_row + tile_rows])
    k_col = np.concatenate([h_block % tile_cols, q_col, h_block % tile_cols])
    band = np.floor_divide(k_row, tile_rows) + 1
    k_meta = np.zeros((8, span), np.int32)
    k_meta[0], k_meta[1] = k_row, band
    k_meta[2], k_meta[3] = k_row - (band - 1) * tile_rows, k_col
    picks = np.concatenate([h_block * tile_rows + h_row, h_block * tile_rows + h_row + tile_rows - rows])
    perm = (picks[:, None] == ids[None, :]).astype(np.float32)
    depth = GROUP if time_embed.shape[0] % GROUP == 0 else time_embed.shape[0]

    hbm = pl.BlockSpec(memory_space=pltpu.HBM)
    others = max(n_tw - 1, 1)
    dma = pltpu.SemaphoreType.DMA
    out = pl.pallas_call(
        functools.partial(kernel, (n_th, n_tw, chunks, lanes, tokens, halo, tile_cols, wide, flat)),
        out_shape=pltpu.VMEM(out_form, jnp.bfloat16),
        in_specs=[hbm] * 10,
        out_specs=hbm,
        scratch_shapes=[
            pltpu.SMEM((2, window_extent.shape[0]), jnp.int32),
            pltpu.SMEM((n_tw, 2, n_th), jnp.int32),
            pltpu.VMEM((time_embed.shape[0] // depth, depth), jnp.bfloat16),
            pltpu.VMEM(q_meta.shape, jnp.int32),
            pltpu.VMEM(k_meta.shape, jnp.int32),
            pltpu.VMEM(perm.shape, jnp.bfloat16),
            pltpu.VMEM((chunks, n_tw, tokens, lanes), jnp.bfloat16),
            pltpu.VMEM((chunks, n_tw, 2, span, lanes), jnp.bfloat16),
            pltpu.VMEM((chunks, n_tw, 2, 2 * halo, lanes), jnp.bfloat16),
            pltpu.VMEM((chunks, n_tw, tokens, lanes), jnp.bfloat16),
            pltpu.VMEM((text_kv.shape[1], 2, text_kv.shape[2]), jnp.bfloat16),
            pltpu.VMEM((chunks, 2, -(-text_kv.shape[1] // GROUP) * GROUP, lanes), jnp.bfloat16),
            pltpu.VMEM(gate_weight.shape, jnp.bfloat16),
            pltpu.VMEM((chunks, 1, lanes), jnp.float32),
            pltpu.VMEM((n_tw, HALO * HALO, tokens, wide * span), jnp.float32),
            dma((1,)),
            dma((others,)),
            pltpu.VMEM((tokens, lanes), jnp.bfloat16),
        ],
        compiler_params=pltpu.CompilerParams(
            collective_id=0, has_side_effects=True, vmem_limit_bytes=56 * 1024 * 1024
        ),
    )(
        window_extent.T,
        tile_valid.transpose(1, 2, 0),
        q,
        kv,
        text_kv.transpose(1, 0, 2),
        time_embed.reshape(-1, depth),
        gate_weight,
        jnp.asarray(q_meta),
        jnp.asarray(k_meta),
        jnp.asarray(perm, jnp.bfloat16),
    )
    if not flat:
        out = out.transpose(2, 0, 1, 3)
    return out.reshape(frames, tile_cols, tile_rows, model_width).transpose(0, 2, 1, 3)


def solution(mesh):
    placed = (
        P("vid", "th", "tw", None),
        P(None, "vid", "th", "tw", None),
        P(None, "vid", "tw"),
        P("vid"),
        P(None, "tw"),
        P(),
        P("vid", None, None),
    )
    return jax.shard_map(
        functools.partial(body, (mesh.shape["th"], mesh.shape["tw"])),
        mesh=mesh,
        in_specs=placed,
        out_specs=P("vid", "th", "tw", None),
        check_vma=False,
    )
```

time: 30.5 us -> 29.9 us (0.980)
  Pallas kernels: 29.5 us -> 28.8 us
    pallas_call x1, Pallas kernels: 29.5 us -> 28.8 us  [body(): pl.pallas_call(functools.partial(kernel, (n_th, n_tw, chunks, lanes, toke...]
where the time goes in v7:
time: 29.9 us; the launch traced here: 29.7 us
  Pallas kernels  28.8 us (96%)
  local copies, waits for them, and re-layouts  0.82 us (3%)
    pallas_call x1, Pallas kernels, body(): pl.pallas_call(functools.partial(kernel, (n_th, n_tw, chunks, lanes, toke...  28.8 us
    unnamed x1, local copies, waits for them, and re-layouts  0.82 us

profile of v7, /device:TPU:1, one launch (start us, length us, event | category | flops | bytes accessed | tf_op | source)
XLA Modules:
  0.0 29.7 jit_solution(6007859267589318631)
XLA Ops:
  0.0 28.8 %shard_map.100 = bf16[96,3072]{1,0:T(8,128)(2,1)S(1)} custom-call(s32[2,48]{1,0:T(2,128)} %bitcast.18, s32[2,2,4]{2,1,0:T(2,128)} %bitcast.17, bf16[96,3072]{1,0:T(8,128)(2,1)} %bitcast.16, bf16[2,96,3072]{2,1,0:T(8,128)(2,1)} %bitcast.15, bf16[226,2,1536]{2,1,0:T(2,128)(2,1)} %bitcast.14, bf16[4,128]{1,0:T(4,128)(2,1)} %bitcast.19, ...), custom_call_target="tpu_custom_call" | custom-call | tf_op jit(solution)/shard_map/pallas_call | solution.py:475
  28.9 0.8 %copy.12 = bf16[4,8,3,3072]{3,1,2,0:T(8,128)(2,1)} copy(bf16[4,8,3,3072]{3,1,2,0:T(8,128)(2,1)S(1)} %bitcast.13) | data formatting | bytes 1179648

commit v8 on v7

--- a/solution.py
+++ b/solution.py
@@ -152,20 +152,6 @@
         def _():
             pl.semaphore_signal(barrier, inc=1, device_id={"th": th + 1}, device_id_type=MESH)
 
-        pl.semaphore_wait(barrier, n_tw - 1 + has_up.astype(jnp.int32) + has_down.astype(jnp.int32))
-
-        for c in range(chunks + behind):
-            for i in range(1, n_tw):
-                if c < chunks:
-                    kv_copy(c, i, tw).start()
-                if c >= behind and not (detour and c - behind == astray):
-                    q_copy(c - behind, i, tw).start()
-            if detour and c - behind == astray:
-
-                @pl.when(th != 0)
-                def _():
-                    q_copy(astray, 1, tw).start()
-
         gw_load = pltpu.make_async_copy(gw_in, gw_ref, load_sem.at[0])
         text_load = pltpu.make_async_copy(text_in, text_raw, load_sem.at[1])
         for c in range(chunks):
@@ -188,6 +174,20 @@
             load.start()
         gw_load.start()
         text_load.start()
+
+        pl.semaphore_wait(barrier, n_tw - 1 + has_up.astype(jnp.int32) + has_down.astype(jnp.int32))
+
+        for c in range(chunks + behind):
+            for i in range(1, n_tw):
+                if c < chunks:
+                    kv_copy(c, i, tw).start()
+                if c >= behind and not (detour and c - behind == astray):
+                    q_copy(c - behind, i, tw).start()
+            if detour and c - behind == astray:
+
+                @pl.when(th != 0)
+                def _():
+                    q_copy(astray, 1, tw).start()
 
         @pl.when(jnp.logical_not(has_up))
         def _():

time: 29.9 us -> 29.9 us (level)
  no operation moved by 1% of the time
where the time goes in v8:
time: 29.9 us; the launch traced here: 29.7 us
  Pallas kernels  28.9 us (97%)
  local copies, waits for them, and re-layouts  0.82 us (3%)
    pallas_call x1, Pallas kernels, body(): pl.pallas_call(functools.partial(kernel, (n_th, n_tw, chunks, lanes, toke...  28.9 us
    unnamed x1, local copies, waits for them, and re-layouts  0.82 us

profile of v8, /device:TPU:1, one launch (start us, length us, event | category | flops | bytes accessed | tf_op | source)
XLA Modules:
  0.0 29.7 jit_solution(11233332558215493425)
XLA Ops:
  0.0 28.9 %shard_map.100 = bf16[96,3072]{1,0:T(8,128)(2,1)S(1)} custom-call(s32[2,48]{1,0:T(2,128)} %bitcast.18, s32[2,2,4]{2,1,0:T(2,128)} %bitcast.17, bf16[96,3072]{1,0:T(8,128)(2,1)} %bitcast.16, bf16[2,96,3072]{2,1,0:T(8,128)(2,1)} %bitcast.15, bf16[226,2,1536]{2,1,0:T(2,128)(2,1)} %bitcast.14, bf16[4,128]{1,0:T(4,128)(2,1)} %bitcast.19, ...), custom_call_target="tpu_custom_call" | custom-call | tf_op jit(solution)/shard_map/pallas_call | solution.py:475
  28.9 0.8 %copy.12 = bf16[4,8,3,3072]{3,1,2,0:T(8,128)(2,1)} copy(bf16[4,8,3,3072]{3,1,2,0:T(8,128)(2,1)S(1)} %bitcast.13) | data formatting | bytes 1179648

commit v9 on v8

--- a/solution.py
+++ b/solution.py
@@ -71,7 +71,7 @@
     def all_of(ref, sem):
         pltpu.make_async_copy(ref, ref, sem).wait()
 
-    behind = max(chunks - 2, 0)
+    behind = max(chunks - 3, 0)
     lag = min(2, chunks)
     early = max(0, chunks - 1 - lag)
     detour = n_tw == 2 and n_th >= 4 and early > 2 and chunks > behind + 1

time: 29.9 us -> 29.9 us (level)
  no operation moved by 1% of the time
where the time goes in v9:
time: 29.9 us; the launch traced here: 29.7 us
  Pallas kernels  28.9 us (97%)
  local copies, waits for them, and re-layouts  0.82 us (3%)
    pallas_call x1, Pallas kernels, body(): pl.pallas_call(functools.partial(kernel, (n_th, n_tw, chunks, lanes, toke...  28.9 us
    unnamed x1, local copies, waits for them, and re-layouts  0.82 us

profile of v9, /device:TPU:1, one launch (start us, length us, event | category | flops | bytes accessed | tf_op | source)
XLA Modules:
  0.0 29.7 jit_solution(10813059296271945337)
XLA Ops:
  0.0 28.9 %shard_map.100 = bf16[96,3072]{1,0:T(8,128)(2,1)S(1)} custom-call(s32[2,48]{1,0:T(2,128)} %bitcast.18, s32[2,2,4]{2,1,0:T(2,128)} %bitcast.17, bf16[96,3072]{1,0:T(8,128)(2,1)} %bitcast.16, bf16[2,96,3072]{2,1,0:T(8,128)(2,1)} %bitcast.15, bf16[226,2,1536]{2,1,0:T(2,128)(2,1)} %bitcast.14, bf16[4,128]{1,0:T(4,128)(2,1)} %bitcast.19, ...), custom_call_target="tpu_custom_call" | custom-call | tf_op jit(solution)/shard_map/pallas_call | solution.py:475
  28.9 0.8 %copy.12 = bf16[4,8,3,3072]{3,1,2,0:T(8,128)(2,1)} copy(bf16[4,8,3,3072]{3,1,2,0:T(8,128)(2,1)S(1)} %bitcast.13) | data formatting | bytes 1179648
